TPU v7x, 128 devices: a whole 4x4x4 slice. The times are simulated.
128 devices in a mesh: grp: 4 (over z_lo, core), dp: 32 (over z_hi, y, x).
Axes of the slice: x: 4, y: 4, z: 4 (z_hi: 2, z_lo: 2; z = z_hi * 2 + z_lo), core: 2. Of those that a mesh axis runs over, the one named last changes fastest.
Arguments:
- activations: bfloat16 [262144, 1280], P(('grp', 'dp')), may hold values from -6 to 6
- cotangent: bfloat16 [262144, 1280], P(('grp', 'dp')), may hold values from -0.01171875 to 0.01171875
- carried_error: float32 [128, 1280, 1280], P(('grp', 'dp')), may hold values from -6 to 6
- owner_error: float32 [1280, 1280], P(('grp', 'dp')), may hold values from -6 to 6
Outputs:
- update: float32 [1280, 1280], replicated
All inputs are finite; a program needn't handle non-finite values.
Results may differ from a plain program's by a relative error of at most 0.012.
Values may be sent and summed in bfloat16 or wider, within the bound.
A program may use at most 128 MiB of HBM per device.

v0:
```python
import jax
import jax.numpy as jnp
from jax import lax
from jax.sharding import PartitionSpec as P

D = 1280
BLOCK = 128


def cut_along(value, dim, devices):
    shape = value.shape
    parts = value.reshape(*shape[:dim], devices, shape[dim] // devices, *shape[dim + 1 :])
    return jnp.moveaxis(parts, dim, 0)


def sent_and_summed(value, axis, dim):
    devices = lax.axis_size(axis)
    parts = lax.all_to_all(cut_along(value, dim, devices), axis, 0, 0, tiled=True)
    return jnp.sum(parts, axis=0)


def side_by_side(arrays, axis, dim, along):
    ends, at = ([], 0)
    for a in arrays[:-1]:
        at += a.shape[along]
        ends.append(at)
    both = jnp.concatenate(arrays, axis=along)
    return tuple(jnp.split(lax.all_gather(both, axis, axis=dim, tiled=True), ends, axis=along))


def quantize(values):
    blocks = values.reshape(values.shape[:-1] + (values.shape[-1] // BLOCK, BLOCK))
    largest = jnp.max(jnp.abs(blocks), axis=-1)
    scales = ((largest + 1e-06) / 127.0).astype(jnp.bfloat16)
    levels = (blocks / scales.astype(jnp.float32)[..., None]).astype(jnp.bfloat16)
    return (levels.reshape(values.shape), scales)


def dequantize(levels, scales):
    blocks = levels.reshape(levels.shape[:-1] + (levels.shape[-1] // BLOCK, BLOCK)).astype(
        jnp.float32
    )
    return (blocks * scales.astype(jnp.float32)[..., None]).reshape(levels.shape)


def on_device(activations, cotangent, carried_error, owner_error):
    gradient = lax.dot_general(
        activations, cotangent, (((0,), (0,)), ((), ())), preferred_element_type=jnp.float32
    )
    levels, scales = quantize(gradient + carried_error[0])
    grp_count = lax.axis_size("grp")
    dp_count = lax.axis_size("dp")
    owner_rows = D // (grp_count * dp_count)
    block_count = D // BLOCK
    got_levels, got_scales = (
        lax.all_to_all(
            levels.reshape(grp_count, dp_count, owner_rows, D),
            "dp",
            split_axis=1,
            concat_axis=1,
            tiled=True,
        ),
        lax.all_to_all(
            scales.reshape(grp_count, dp_count, owner_rows, block_count),
            "dp",
            split_axis=1,
            concat_axis=1,
            tiled=True,
        ),
    )
    partial_value = jnp.sum(dequantize(got_levels, got_scales), axis=1)
    summed = sent_and_summed(partial_value, "grp", 0)[0]
    summed = summed + owner_error
    owner_level, owner_scale = quantize(summed)
    all_levels, all_scales = side_by_side((owner_level, owner_scale), ("grp", "dp"), 0, 1)
    return dequantize(all_levels, all_scales)


def solution(mesh):
    return jax.shard_map(
        on_device,
        mesh=mesh,
        in_specs=(
            P(("grp", "dp"), None),
            P(("grp", "dp"), None),
            P(("grp", "dp"), None, None),
            P(("grp", "dp"), None),
        ),
        out_specs=P(),
        check_vma=False,
    )
```

profile of v0, /device:TPU:1, one launch (start us, length us, event | category | flops | bytes accessed | tf_op | source)
XLA Modules:
  0.0 499.8 jit_solution(17454378079995790397)
XLA Ops:
  6.5 14.4 %fusion.1 = (f32[1280,1280]{1,0:T(8,128)}, f32[1280,1280]{1,0:T(8,128)}) fusion(f32[1,1280,1280]{2,1,0:T(8,128)} %param.6, bf16[2048,1280]{1,0:T(8,128)(2,1)} %param.4, bf16[2048,1280]{1,0:T(8,128)(2,1)} %param.5), kind=kOutput, calls=%fused_computation.9 | convolution fusion | flops 6714163200 | bytes 30146560 | tf_op jit(solution)/shard_map/dot_general | solution.py:47
  21.0 8.2 %copy.38 = f32[1280,1280]{0,1:T(8,128)} copy(f32[1280,1280]{1,0:T(8,128)} %get-tuple-element.7) | data formatting | bytes 13107200 | tf_op jit(solution)/shard_map/abs | solution.py:33
  29.1 3.3 reduce_max.18
  32.4 0.7 convert_element_type.58
  33.1 0.2 copy.55
  33.3 0.9 reshape.46
  34.2 11.4 %all-to-all-start.1 = ((bf16[32,2,200]{2,1,0:T(2,128)(2,1)}), bf16[32,2,200]{2,1,0:T(2,128)(2,1)S(1)}, u32[]{:S(2)}, u32[]{:S(2)}) async-start(bf16[32,2,200]{2,1,0:T(2,128)(2,1)} %reshape.46), calls=%async_computation.1 | async-start | bytes 65536 | tf_op jit(solution)/shard_map/all_to_all | solution.py:63
  45.6 0.2 copy.39
  45.8 8.1 %div.36 = f32[1280,10,128]{2,1,0:T(8,128)} broadcast(f32[1280,10]{1,0:T(8,128)S(1)} %copy.39), dimensions={0,1} | broadcast | bytes 6604800 | tf_op jit(solution)/shard_map/div | solution.py:35
  53.9 11.4 %div.37 = f32[4,32,10,1280]{3,2,1,0:T(8,128)} reshape(f32[1280,10,128]{2,1,0:T(8,128)} %div.36) | data formatting | bytes 13107200 | tf_op jit(solution)/shard_map/div | solution.py:35
  65.3 8.6 %reshape.42 = f32[4,32,10,1280]{3,2,1,0:T(8,128)} reshape(f32[1280,1280]{1,0:T(8,128)} %get-tuple-element.8) | data formatting | bytes 13107200 | tf_op jit(solution)/shard_map/reshape | solution.py:32
  74.0 11.4 %divide_convert_fusion = bf16[4,32,10,1280]{3,2,1,0:T(8,128)(2,1)} fusion(f32[4,32,10,1280]{3,2,1,0:T(8,128)} %reshape.42, f32[4,32,10,1280]{3,2,1,0:T(8,128)} %div.37), kind=kLoop, calls=%fused_computation | loop fusion | flops 3276800 | bytes 16384000 | tf_op jit(solution)/shard_map/convert_element_type | solution.py:35
  85.3 6.8 %copy.40 = bf16[4,32,10,1280]{3,0,2,1:T(4,128)(2,1)} copy(bf16[4,32,10,1280]{3,2,1,0:T(8,128)(2,1)} %divide_convert_fusion) | data formatting | bytes 6553600 | tf_op jit(solution)/shard_map/convert_element_type | solution.py:35
  92.1 0.0 all-to-all-done.1
  92.1 9.1 %all-to-all-start = ((bf16[4,32,10,1280]{3,0,2,1:T(4,128)(2,1)}), bf16[4,32,10,1280]{3,0,2,1:T(4,128)(2,1)S(1)}, u32[]{:S(2)}, u32[]{:S(2)}) async-start(bf16[4,32,10,1280]{3,0,2,1:T(4,128)(2,1)} %copy.40), calls=%async_computation | async-start | bytes 6553600 | tf_op jit(solution)/shard_map/all_to_all | solution.py:56
  101.2 0.0 all-gather.3.cloned.1.call-start
  101.3 1.0 reshape.47
  102.3 1.3 copy.43
  103.6 1.2 copy.44
  104.8 6.8 %mul.22 = f32[4,32,10,10,128]{4,3,1,2,0:T(8,128)} broadcast(f32[4,32,10,10]{3,1,2,0:T(8,128)} %copy.44), dimensions={0,1,2,3} | broadcast | bytes 6604800 | tf_op jit(solution)/shard_map/mul | solution.py:43
  111.5 9.1 %mul.23 = f32[4,32,10,1280]{3,1,2,0:T(8,128)} reshape(f32[4,32,10,10,128]{4,3,1,2,0:T(8,128)} %mul.22) | data formatting | bytes 13107200 | tf_op jit(solution)/shard_map/mul | solution.py:43
  120.6 0.0 copy-start
  120.7 20.9 %all-to-all-done = bf16[4,32,10,1280]{3,0,2,1:T(4,128)(2,1)S(1)} async-done(((bf16[4,32,10,1280]{3,0,2,1:T(4,128)(2,1)}), bf16[4,32,10,1280]{3,0,2,1:T(4,128)(2,1)S(1)}, u32[]{:S(2)}, u32[]{:S(2)}) %all-to-all-start) | async-done | bytes 3276832 | tf_op jit(solution)/shard_map/all_to_all | solution.py:56
  141.6 4.4 multiply_reduce_fusion
  146.0 0.2 copy.46
  146.2 10.1 %all_to_all.15 = f32[4,1,10,1280]{3,1,2,0:T(1,128)S(1)} all-to-all(f32[4,1,10,1280]{3,1,2,0:T(1,128)S(1)} %copy.46), channel_id=1, replica_groups=mesh['grp'=4,'dp'=32] {'grp'}, dimensions={0} | all-to-all | bytes 409600 | tf_op jit(solution)/shard_map/all_to_all | solution.py:18
  156.4 0.2 reduce_sum.19
  156.6 0.0 copy-done
  156.6 0.1 reduce_max.19
  156.7 0.1 div.41
  156.9 0.6 maximum_bitcast_fusion
  157.5 0.0 all-gather.3.cloned.1.call-update
  157.6 307.8 %all-gather.3.cloned.1.call-done = bf16[128,10,1290]{2,1,0:T(8,128)(2,1)} async-done(((bf16[1,10,1290]{2,1,0:T(8,128)(2,1)}), bf16[128,10,1290]{2,1,0:T(8,128)(2,1)}) %all-gather.3.cloned.1.call-update) | async-done | bytes 3302416 | tf_op jit(solution)/shard_map/all_gather | solution.py:28
  465.4 7.7 %reshape.45 = bf16[1280,1290]{1,0:T(8,128)(2,1)} reshape(bf16[128,10,1290]{2,1,0:T(8,128)(2,1)} %all-gather.3.cloned.1.call-done) | data formatting | bytes 6604800
  473.1 1.0 split.9
  474.1 0.2 copy.51
  474.2 3.3 mul.25
  477.5 8.2 %copy.48 = f32[1280,1280]{1,0:T(8,128)} copy(f32[1280,1280]{0,1:T(8,128)} %bitcast.21) | data formatting | bytes 13107200 | tf_op jit(solution)/shard_map/mul | solution.py:43
  485.7 7.2 %convert_multiply_fusion = f32[1280,1280]{1,0:T(8,128)} fusion(f32[1280,1280]{1,0:T(8,128)} %copy.48, bf16[1280,1290]{1,0:T(8,128)(2,1)} %reshape.45), kind=kLoop, calls=%fused_computation.2 | loop fusion | flops 3276800 | bytes 16384000 | tf_op jit(solution)/shard_map/mul | solution.py:43
  (7 shorter events, 0.1 us)
Async XLA Ops:
  34.2 57.9 %all-to-all-start.1 = ((bf16[32,2,200]{2,1,0:T(2,128)(2,1)}), bf16[32,2,200]{2,1,0:T(2,128)(2,1)S(1)}, u32[]{:S(2)}, u32[]{:S(2)}) async-start(bf16[32,2,200]{2,1,0:T(2,128)(2,1)} %reshape.46), calls=%async_computation.1 | async-start | bytes 65536 | tf_op jit(solution)/shard_map/all_to_all | solution.py:63
  92.1 49.4 %all-to-all-start = ((bf16[4,32,10,1280]{3,0,2,1:T(4,128)(2,1)}), bf16[4,32,10,1280]{3,0,2,1:T(4,128)(2,1)S(1)}, u32[]{:S(2)}, u32[]{:S(2)}) async-start(bf16[4,32,10,1280]{3,0,2,1:T(4,128)(2,1)} %copy.40), calls=%async_computation | async-start | bytes 6553600 | tf_op jit(solution)/shard_map/all_to_all | solution.py:56
  101.2 364.1 %all-gather.3.cloned.1.call-start = ((), (), s32[]{:S(2)}) async-start(), calls=%async_computation.3 | async-start | bytes 5812224 | tf_op jit(solution)/shard_map/all_gather | solution.py:28
  120.6 35.9 %copy-start = (f32[10,1280]{1,0:T(8,128)S(1)}, f32[10,1280]{1,0:T(8,128)}, u32[]{:S(2)}) copy-start(f32[10,1280]{1,0:T(8,128)} %param.7) | copy-start | bytes 153604
Sparse Core Ops, SparseCore 0:
  157.7 307.6 all-gather.2
where the time goes:
time: 501 us; the launch traced here: 500 us
  waiting for transfers between devices  329 us (66%)
  local copies, waits for them, and re-layouts  85.1 us (17%)
  other arithmetic  27.3 us (5%)
  starting transfers between devices  20.5 us (4%)
  matrix products  14.4 us (3%)
  between operations  13.5 us (3%)
  blocking collectives  10.1 us (2%)
    all_gather x1, waiting for transfers between devices, side_by_side(): lax.all_gather(both, axis, axis=dim, tiled=True)  308 us
    mul x4, local copies, waits for them, and re-layouts, dequantize(): blocks * scales.astype(jnp.float32)[..., None]  27.3 us
    all_to_all x1, waiting for transfers between devices, on_device(): lax.all_to_all(levels.reshape(grp_count, dp_count, owner_rows, D), 'dp',...  20.9 us
    div x3, local copies, waits for them, and re-layouts, quantize(): blocks / scales.astype(jnp.float32)[..., None]  19.6 us
    dot_general x1, matrix products, on_device(): lax.dot_general(activations, cotangent, (((0,), (0,)), ((), ())), preferr...  14.4 us
    convert_element_type x2, other arithmetic, quantize(): (blocks / scales.astype(jnp.float32)[..., None]).astype(jnp.bfloat16)  11.4 us
    all_to_all x1, starting transfers between devices, on_device(): lax.all_to_all(scales.reshape(grp_count, dp_count, owner_rows, block_coun...  11.4 us
    all_to_all x1, blocking collectives, sent_and_summed(): lax.all_to_all(cut_along(value, dim, devices), axis, 0, 0, tiled=True)  10.1 us
  transfers between devices with their start and end apart: 3, of which 2 were waited for; matrix products, arithmetic and copies ran while one was open for 13% of the time, Pallas kernels for 0%

commit v1 on v0

v1 whole, which is shorter than its diff:
```python
import jax
import jax.numpy as jnp
from jax import lax
from jax.sharding import PartitionSpec as P

D = 1280
BLOCK = 128


def quantize(values):
    blocks = values.reshape(values.shape[:-1] + (values.shape[-1] // BLOCK, BLOCK))
    largest = jnp.max(jnp.abs(blocks), axis=-1)
    scales = ((largest + 1e-06) / 127.0).astype(jnp.bfloat16)
    levels = (blocks / scales.astype(jnp.float32)[..., None]).astype(jnp.bfloat16)
    return (levels.reshape(values.shape), scales)


def dequantize(levels, scales):
    blocks = levels.reshape(levels.shape[:-1] + (levels.shape[-1] // BLOCK, BLOCK)).astype(
        jnp.float32
    )
    return (blocks * scales.astype(jnp.float32)[..., None]).reshape(levels.shape)


def on_device(activations, cotangent, carried_error, owner_error):
    gradient = lax.dot_general(
        activations, cotangent, (((0,), (0,)), ((), ())), preferred_element_type=jnp.float32
    )
    own = dequantize(*quantize(gradient + carried_error[0]))
    rows = owner_error.shape[0]
    start = rows * (lax.axis_index("grp") * lax.axis_size("dp") + lax.axis_index("dp"))
    mine = lax.dynamic_slice_in_dim(own, start, rows, 0) + owner_error
    own = lax.dynamic_update_slice_in_dim(own, mine, start, 0)
    summed = lax.psum(own.astype(jnp.bfloat16), ("grp", "dp")).astype(jnp.float32)
    return dequantize(*quantize(summed))


def solution(mesh):
    return jax.shard_map(
        on_device,
        mesh=mesh,
        in_specs=(
            P(("grp", "dp"), None),
            P(("grp", "dp"), None),
            P(("grp", "dp"), None, None),
            P(("grp", "dp"), None),
        ),
        out_specs=P(),
        check_vma=False,
    )
```

time: 501 us -> 258 us (0.51)
  waiting for transfers between devices: 329 us -> 156 us
  local copies, waits for them, and re-layouts: 85.1 us -> 41 us
  starting transfers between devices: 20.5 us -> 0.01 us
  blocking collectives: 10.1 us -> 0 us
  other arithmetic: 27.3 us -> 32.6 us
    all_gather x1 -> x0, waiting for transfers between devices: 308 us -> none  [side_by_side(): lax.all_gather(both, axis, axis=dim, tiled=True)]
    psum x0 -> x1, waiting for transfers between devices: none -> 156 us  [on_device(): lax.psum(own.astype(jnp.bfloat16), ('grp', 'dp')).astype(jnp.float32)]
    mul x4 -> x0, local copies, waits for them, and re-layouts: 27.3 us -> none  [dequantize(): blocks * scales.astype(jnp.float32)[..., None]]
    all_to_all x2 -> x0, waiting for transfers between devices: 20.9 us -> none  [the longest x1 20.9 us: on_device(): lax.all_to_all(levels.reshape(grp_count, dp_count, owner_rows, D), 'dp',...]
    all_to_all x2 -> x0, starting transfers between devices: 20.4 us -> none  [the longest x1 11.4 us: on_device(): lax.all_to_all(scales.reshape(grp_count, dp_count, owner_rows, block_coun...]
    all_to_all x1 -> x0, blocking collectives: 10.1 us -> none  [sent_and_summed(): lax.all_to_all(cut_along(value, dim, devices), axis, 0, 0, tiled=True)]
    unnamed x8 -> x4, local copies, waits for them, and re-layouts: 9.8 us -> 0.01 us
    convert_element_type x5 -> x0, local copies, waits for them, and re-layouts: 9.03 us -> none  [the longest x1 6.8 us: quantize(): (blocks / scales.astype(jnp.float32)[..., None]).astype(jnp.bfloat16)]
  transfers between devices with their start and end apart: 3 -> 1, of which waited for: 2 -> 1; matrix products, arithmetic and copies ran while one was open for 13% -> 0% of each run, Pallas kernels for 0% -> 0%
where the time goes in v1:
time: 258 us; the launch traced here: 257 us
  waiting for transfers between devices  156 us (60%)
  local copies, waits for them, and re-layouts  41 us (16%)
  other arithmetic  32.6 us (13%)
  matrix products  14.4 us (6%)
  between operations  13.4 us (5%)
    psum x1, waiting for transfers between devices, on_device(): lax.psum(own.astype(jnp.bfloat16), ('grp', 'dp')).astype(jnp.float32)  156 us
    div x4, local copies, waits for them, and re-layouts, quantize(): blocks / scales.astype(jnp.float32)[..., None]  23.1 us
    abs x2, local copies, waits for them, and re-layouts, quantize(): largest = jnp.max(jnp.abs(blocks), axis=-1)  16.3 us
    mul x2, other arithmetic, dequantize(): blocks * scales.astype(jnp.float32)[..., None]  14.9 us
    dot_general x1, matrix products, on_device(): lax.dot_general(activations, cotangent, (((0,), (0,)), ((), ())), preferr...  14.4 us
    reduce_max x2, other arithmetic, quantize(): largest = jnp.max(jnp.abs(blocks), axis=-1)  6.56 us
    abs x1, other arithmetic, quantize(): largest = jnp.max(jnp.abs(blocks), axis=-1)  5.29 us
  transfers between devices with their start and end apart: 1, of which 1 were waited for; matrix products, arithmetic and copies ran while one was open for 0% of the time, Pallas kernels for 0%

profile of v1, /device:TPU:1, one launch (start us, length us, event | category | flops | bytes accessed | tf_op | source)
XLA Modules:
  0.0 257.3 jit_solution(2272758399839218393)
XLA Ops:
  6.5 0.0 all-reduce.2.cloned.1.call-start
  6.5 14.4 %fusion.3 = (f32[1280,1280]{1,0:T(8,128)}, f32[1280,1280]{1,0:T(8,128)}) fusion(f32[1,1280,1280]{2,1,0:T(8,128)} %param.6, bf16[2048,1280]{1,0:T(8,128)(2,1)} %param.4, bf16[2048,1280]{1,0:T(8,128)(2,1)} %param.5), kind=kOutput, calls=%fused_computation.12 | convolution fusion | flops 6714163200 | bytes 30146560 | tf_op jit(solution)/shard_map/dot_general | solution.py:26
  21.0 8.2 %copy.5 = f32[1280,1280]{0,1:T(8,128)} copy(f32[1280,1280]{1,0:T(8,128)} %get-tuple-element.5) | data formatting | bytes 13107200 | tf_op jit(solution)/shard_map/abs | solution.py:12
  29.1 3.3 %reduce_max.18 = f32[1280,10]{0,1:T(8,128)S(1)} reduce(f32[1280,10,128]{0,2,1:T(8,128)} %bitcast.9, f32[]{:T(128)} %constant.5.clone.1), dimensions={2}, to_apply=%region_0.0 | reduce | flops 1625600 | bytes 6604804 | tf_op jit(solution)/shard_map/reduce_max | solution.py:12
  32.4 3.3 %div.29 = f32[1280,10,128]{0,2,1:T(8,128)} broadcast(f32[1280,10]{0,1:T(8,128)S(1)} %fusion.1), dimensions={0,1} | broadcast | bytes 6604800 | tf_op jit(solution)/shard_map/div | solution.py:14
  35.7 8.2 %copy.6 = f32[1280,1280]{1,0:T(8,128)} copy(f32[1280,1280]{0,1:T(8,128)} %bitcast.10) | data formatting | bytes 13107200 | tf_op jit(solution)/shard_map/div | solution.py:14
  43.9 0.0 copy-start.1
  43.9 8.4 %convert_multiply_fusion.1 = f32[1280,1280]{1,0:T(8,128)} fusion(f32[1280,1280]{1,0:T(8,128)} %copy.6, f32[1280,1280]{1,0:T(8,128)} %get-tuple-element.6), kind=kLoop, calls=%fused_computation.5 | loop fusion | flops 6553600 | bytes 19660800 | tf_op jit(solution)/shard_map/mul | solution.py:22
  52.3 0.0 copy-done.1
  52.3 0.9 dynamic-slice_add_fusion
  53.2 1.6 dynamic_update_slice.3
  54.8 4.9 %convert_element_type.56 = bf16[1280,1280]{1,0:T(8,128)(2,1)} convert(f32[1280,1280]{1,0:T(8,128)} %dynamic_update_slice.3) | non-fusion elementwise | flops 1638400 | bytes 9830400 | tf_op jit(solution)/shard_map/convert_element_type | solution.py:34
  59.7 0.0 all-reduce.2.cloned.1.call-update
  59.7 155.8 %all-reduce.2.cloned.1.call-done = bf16[1280,1280]{1,0:T(8,128)(2,1)} async-done(((bf16[1280,1280]{1,0:T(8,128)(2,1)}), bf16[1280,1280]{1,0:T(8,128)(2,1)}) %all-reduce.2.cloned.1.call-update) | async-done | bytes 3276816 | tf_op jit(solution)/shard_map/psum | solution.py:34
  215.6 5.3 %convert_abs_fusion = f32[1280,1280]{1,0:T(8,128)} fusion(bf16[1280,1280]{1,0:T(8,128)(2,1)} %all-reduce.2.cloned.1.call-done), kind=kLoop, calls=%fused_computation.2 | loop fusion | flops 3276800 | bytes 9830400 | tf_op jit(solution)/shard_map/abs | solution.py:12
  220.9 8.2 %copy.8 = f32[1280,1280]{0,1:T(8,128)} copy(f32[1280,1280]{1,0:T(8,128)} %convert_abs_fusion) | data formatting | bytes 13107200 | tf_op jit(solution)/shard_map/abs | solution.py:12
  229.0 3.3 %reduce_max.19 = f32[1280,10]{0,1:T(8,128)S(1)} reduce(f32[1280,10,128]{0,2,1:T(8,128)} %bitcast.8, f32[]{:T(128)} %constant.5.clone.1), dimensions={2}, to_apply=%region_2.0 | reduce | flops 1625600 | bytes 6604804 | tf_op jit(solution)/shard_map/reduce_max | solution.py:12
  232.3 3.3 %div.33 = f32[1280,10,128]{0,2,1:T(8,128)} broadcast(f32[1280,10]{0,1:T(8,128)S(1)} %fusion.2), dimensions={0,1} | broadcast | bytes 6604800 | tf_op jit(solution)/shard_map/div | solution.py:14
  235.6 0.0 copy-start
  235.6 8.3 %copy.9 = f32[1280,1280]{1,0:T(8,128)} copy(f32[1280,1280]{0,1:T(8,128)} %bitcast.11) | data formatting | bytes 13107200 | tf_op jit(solution)/shard_map/div | solution.py:14
  243.9 0.0 copy-done
  243.9 6.5 %convert_multiply_fusion = f32[1280,1280]{1,0:T(8,128)} fusion(f32[1280,1280]{1,0:T(8,128)} %copy.9, bf16[1280,1280]{1,0:T(8,128)(2,1)S(1)} %copy-done), kind=kLoop, calls=%fused_computation.4 | loop fusion | flops 8192000 | bytes 16384000 | tf_op jit(solution)/shard_map/mul | solution.py:22
  (2 shorter events, 0.0 us)
Async XLA Ops:
  6.5 209.0 %all-reduce.2.cloned.1.call-start = ((), (), s32[]{:S(2)}) async-start(), calls=%async_computation | async-start | bytes 6553600 | tf_op jit(solution)/shard_map/psum | solution.py:34
  43.9 8.4 %copy-start.1 = (f32[10,1280]{1,0:T(8,128)S(1)}, f32[10,1280]{1,0:T(8,128)}, u32[]{:S(2)}) copy-start(f32[10,1280]{1,0:T(8,128)} %param.7) | copy-start | bytes 153604
  235.6 8.3 %copy-start = (bf16[1280,1280]{1,0:T(8,128)(2,1)S(1)}, bf16[1280,1280]{1,0:T(8,128)(2,1)}, u32[]{:S(2)}) copy-start(bf16[1280,1280]{1,0:T(8,128)(2,1)} %all-reduce.2.cloned.1.call-done) | copy-start | bytes 9830404
Sparse Core Ops, SparseCore 0:
  59.9 155.6 all-reduce.1

commit v2 on v1

v2 whole, which is shorter than its diff:
```python
import jax
import jax.numpy as jnp
from jax import lax
from jax.experimental import pallas as pl
from jax.experimental.pallas import tpu as pltpu
from jax.sharding import PartitionSpec as P

D = 1280
BLOCK = 128
TOK = 2048
MESH = pl.DeviceIdType.MESH
B = 5
ROWS = D // B
TILES = ROWS // 8
HALF = 5
KS = (3, 3, 2)
OFFS = (0, 12, 24)
KOFF = (0, 3, 6)
ORDER = (("z", "y", "x"), ("y", "x", "z"), ("x", "z", "y"))
GROUPS = ((0, 2), (2, 3))


def quantized(x):
    largest = jnp.max(jnp.abs(x), axis=-1, keepdims=True)
    scale = ((largest + 1e-06) / 127.0).astype(jnp.bfloat16).astype(jnp.float32)
    level = (x * (1.0 / scale)).astype(jnp.bfloat16).astype(jnp.float32)
    return level * scale


def places():
    g, d = lax.axis_index("grp"), lax.axis_index("dp")
    return {
        "core": lax.rem(g, 2),
        "z": 2 * (d // 16) + g // 2,
        "y": lax.rem(d // 4, 4),
        "x": lax.rem(d, 4),
    }


def device_at(place):
    z = place["z"]
    return (2 * lax.rem(z, 2) + place["core"], 16 * (z // 2) + 4 * place["y"] + place["x"])


def along(place, axis, step):
    return {**place, axis: lax.rem(place[axis] + step, 4)}


def reduce_kernel(
    a_hbm, c_hbm, e_hbm, oe_ref, g_ref,
    a_v, c_v, e_v, at_v, pad_v, q, rx0, s, r1, t, r2, v, r3,
    a_sem, c_sem, e_sem, d2d_recv, p1_recv, p2_recv, p3_recv, g3_recv, g2_recv, g1_recv, gd_recv, sent,
):
    me = places()
    core = me["core"]
    partner = {**me, "core": 1 - core}
    peers = [partner] + [along(me, axis, step) for axis in "xyz" for step in (1, 2, 3)]
    barrier = pltpu.get_barrier_semaphore()
    for peer in peers:
        pl.semaphore_signal(barrier, inc=1, device_id=device_at(peer), device_id_type=MESH)

    def load_a(b):
        return pltpu.make_async_copy(a_hbm.at[:, pl.ds(b * ROWS, ROWS)], a_v.at[b], a_sem.at[b])

    def load_e(b):
        return pltpu.make_async_copy(e_hbm.at[0, pl.ds(b * ROWS, ROWS), :], e_v.at[b], e_sem.at[b])

    load_c = pltpu.make_async_copy(c_hbm, c_v, c_sem)
    load_a(0).start()
    load_c.start()
    for b in range(B):
        if b:
            load_a(b).start()
        load_e(b).start()

    def push(src, dst, peer, send, recv):
        pltpu.make_async_remote_copy(
            src_ref=src, dst_ref=dst, send_sem=send, recv_sem=recv,
            device_id=device_at(peer), device_id_type=MESH,
        ).start()

    def landed(ref, sem):
        pltpu.make_async_copy(ref, ref, sem).wait()

    index = lax.axis_index("grp") * 32 + lax.axis_index("dp")
    first_tile = (10 * index) // 8
    shift = 10 * index - 8 * first_tile
    row = lax.broadcasted_iota(jnp.int32, (16, D), 0)
    padded = jnp.zeros((16, D), jnp.float32)
    for r in range(10):
        padded = jnp.where(row == shift + r, oe_ref[r : r + 1, :], padded)
    pad_v[...] = padded

    pl.semaphore_wait(barrier, len(peers))
    load_c.wait()

    def multiply(b):
        load_a(b).wait()
        at_v[...] = a_v[b].T
        load_e(b).wait()
        for n in range(5):
            x = jnp.dot(at_v[...], c_v[:, n * 256 : (n + 1) * 256], preferred_element_type=jnp.float32)
            x = x + e_v[b, :, n * 256 : (n + 1) * 256]
            for u in range(2):
                h, j = divmod(2 * n + u, HALF)
                own = quantized(x[:, u * 128 : (u + 1) * 128])
                q[b, h, :, j] = own.astype(jnp.bfloat16).reshape(TILES, 8, 128)
        for w in range(2):
            tile = first_tile + w

            @pl.when(tile // TILES == b)
            def _():
                i = lax.rem(tile, TILES)
                for h in range(2):
                    for j in range(HALF):
                        col = (h * HALF + j) * 128
                        was = q[b, h, i, j].astype(jnp.float32)
                        q[b, h, i, j] = (was + pad_v[w * 8 : w * 8 + 8, col : col + 128]).astype(jnp.bfloat16)

        push(q.at[b, 1 - core], rx0.at[b], partner, sent.at[0], d2d_recv.at[b])

    def chip_sum(b):
        landed(rx0.at[b], d2d_recv.at[b])
        s[b] = (q[b, core].astype(jnp.float32) + rx0[b].astype(jnp.float32)).astype(jnp.bfloat16)
        for c in range(3):
            for step in (2, 1, 3):
                peer = along(me, ORDER[c][0], step)
                at = OFFS[c] + peer[ORDER[c][0]] * KS[c]
                push(
                    s.at[b, pl.ds(at, KS[c])], r1.at[b, step - 1, pl.ds(KOFF[c], KS[c])],
                    peer, sent.at[1], p1_recv.at[b],
                )

    def first_sum(b):
        landed(r1.at[b], p1_recv.at[b])
        for c in range(3):
            total = s[b, pl.ds(OFFS[c] + me[ORDER[c][0]] * KS[c], KS[c])].astype(jnp.float32)
            for step in range(3):
                total = total + r1[b, step, KOFF[c] : KOFF[c] + KS[c]].astype(jnp.float32)
            t[b, c, 0 : 5 * KS[c]] = total.astype(jnp.bfloat16).reshape(5 * KS[c], 8, 128)

    def second_send(i):
        b, nb = GROUPS[i]
        for c in range(3):
            for step in (2, 1, 3):
                peer = along(me, ORDER[c][1], step)
                push(
                    t.at[pl.ds(b, nb), c, pl.ds(4 * peer[ORDER[c][1]], 4)], r2.at[pl.ds(b, nb), step - 1, c],
                    peer, sent.at[2], p2_recv.at[i],
                )

    def second_sum(i):
        b, nb = GROUPS[i]
        landed(r2.at[pl.ds(b, nb)], p2_recv.at[i])
        for c in range(3):
            total = t[b : b + nb, c, pl.ds(4 * me[ORDER[c][1]], 4)].astype(jnp.float32)
            for step in range(3):
                total = total + r2[b : b + nb, step, c].astype(jnp.float32)
            v[b : b + nb, c] = total.astype(jnp.bfloat16)
        for c in range(3):
            for step in (2, 1, 3):
                peer = along(me, ORDER[c][2], step)
                push(
                    v.at[pl.ds(b, nb), c, peer[ORDER[c][2]]], r3.at[pl.ds(b, nb), step - 1, c],
                    peer, sent.at[3], p3_recv.at[i],
                )

    def spread(i, level, recv):
        b, nb = GROUPS[i]
        for c in range(3):
            p1, p2, p3 = (me[axis] for axis in ORDER[c])
            for step in (2, 1, 3):
                if level == 2:
                    ref = g_ref.at[core, pl.ds(b, nb), c, p1, 4 * p2 + p3]
                elif level == 1:
                    ref = g_ref.at[core, pl.ds(b, nb), c, p1, pl.ds(4 * p2, 4)]
                else:
                    ref = g_ref.at[core, pl.ds(b, nb), c, p1, pl.ds(0, 5 * KS[c])]
                push(ref, ref, along(me, ORDER[c][level], step), sent.at[4 + level], recv)

    def own_update(i):
        b, nb = GROUPS[i]
        landed(r3.at[pl.ds(b, nb)], p3_recv.at[i])
        for c in range(3):
            p1, p2, p3 = (me[axis] for axis in ORDER[c])
            total = v[b : b + nb, c, p3].astype(jnp.float32)
            for step in range(3):
                total = total + r3[b : b + nb, step, c].astype(jnp.float32)
            g_ref[core, b : b + nb, c, p1, 4 * p2 + p3] = quantized(total).astype(jnp.bfloat16)
        spread(i, 2, g3_recv.at[i])

    def gathered(i, level, sem):
        b, nb = GROUPS[i]
        if level == 0:
            landed(r1.at[pl.ds(b, nb)], sem.at[i])
        elif level == 1:
            landed(r2.at[pl.ds(b, nb), :, :, :], sem.at[i])
        else:
            landed(r3.at[pl.ds(b, nb)], sem.at[i])

    def to_partner(i):
        b, nb = GROUPS[i]
        gathered(i, 0, g1_recv)
        push(g_ref.at[core, pl.ds(b, nb)], g_ref.at[core, pl.ds(b, nb)], partner, sent.at[7], gd_recv.at[i])

    def step(b, carry):
        multiply(b)

        @pl.when(b >= 1)
        def _():
            chip_sum(b - 1)

        @pl.when(b >= 3)
        def _():
            first_sum(b - 3)

        return carry

    lax.fori_loop(0, B, step, 0)
    second_send(0)
    chip_sum(B - 1)
    for b in range(2, B):
        first_sum(b)
    second_sum(0)
    second_send(1)
    own_update(0)
    second_sum(1)
    gathered(0, 2, g3_recv)
    spread(0, 1, g2_recv.at[0])
    own_update(1)
    gathered(0, 1, g2_recv)
    spread(0, 0, g1_recv.at[0])
    gathered(1, 2, g3_recv)
    spread(1, 1, g2_recv.at[1])
    gathered(1, 1, g2_recv)
    spread(1, 0, g1_recv.at[1])
    to_partner(0)
    to_partner(1)
    for i, (b, nb) in enumerate(GROUPS):
        landed(g_ref.at[1 - core, pl.ds(b, nb)], gd_recv.at[i])
    landed(rx0, sent.at[0])
    landed(r1, sent.at[1])
    landed(r2, sent.at[2])
    landed(r3, sent.at[3])
    landed(r1, sent.at[4])
    landed(r2, sent.at[5])
    landed(r3, sent.at[6])
    landed(g_ref.at[0], sent.at[7])


def expand_kernel(g_ref, out_ref):
    for h in range(2):
        for c in range(3):
            for a in range(4):
                for k in range(KS[c]):
                    row = 8 * (OFFS[c] + a * KS[c] + k)
                    for j in range(HALF):
                        col = (h * HALF + j) * 128
                        out_ref[row : row + 8, col : col + 128] = g_ref[h, 0, c, a, 5 * k + j].astype(jnp.float32)


def on_device(activations, cotangent, carried_error, owner_error):
    any_spec = pl.BlockSpec(memory_space=pl.ANY)
    bf16, f32, dma = jnp.bfloat16, jnp.float32, pltpu.SemaphoreType.DMA
    shape = (2, B, 3, 4, 16, 8, 128)
    ng = len(GROUPS)
    gathered = pl.pallas_call(
        reduce_kernel,
        out_shape=jax.ShapeDtypeStruct(shape, bf16),
        in_specs=[any_spec, any_spec, any_spec, pl.BlockSpec(memory_space=pltpu.VMEM)],
        out_specs=pl.BlockSpec(memory_space=pltpu.VMEM),
        scratch_shapes=[
            pltpu.VMEM((B, TOK, ROWS), bf16),
            pltpu.VMEM((TOK, D), bf16),
            pltpu.VMEM((B, ROWS, D), f32),
            pltpu.VMEM((ROWS, TOK), bf16),
            pltpu.VMEM((16, D), f32),
            pltpu.VMEM((B, 2, TILES, HALF, 8, 128), bf16),
            pltpu.VMEM((B, TILES, HALF, 8, 128), bf16),
            pltpu.VMEM((B, TILES, HALF, 8, 128), bf16),
            pltpu.VMEM((B, 3, 8, HALF, 8, 128), bf16),
            pltpu.VMEM((B, 3, 16, 8, 128), bf16),
            pltpu.VMEM((B, 3, 3, 4, 8, 128), bf16),
            pltpu.VMEM((B, 3, 4, 8, 128), bf16),
            pltpu.VMEM((B, 3, 3, 8, 128), bf16),
            dma((B,)), dma, dma((B,)), dma((B,)), dma((B,)),
            dma((ng,)), dma((ng,)), dma((ng,)), dma((ng,)), dma((ng,)), dma((ng,)), dma((8,)),
        ],
        compiler_params=pltpu.CompilerParams(
            collective_id=0, has_side_effects=True, vmem_limit_bytes=48 * 2**20
        ),
    )(activations, cotangent, carried_error, owner_error)
    return pl.pallas_call(
        expand_kernel,
        grid=(B,),
        in_specs=[pl.BlockSpec((2, 1, 3, 4, 16, 8, 128), lambda b: (0, b, 0, 0, 0, 0, 0))],
        out_specs=pl.BlockSpec((ROWS, D), lambda b: (b, 0)),
        out_shape=jax.ShapeDtypeStruct((D, D), f32),
        compiler_params=pltpu.CompilerParams(vmem_limit_bytes=16 * 2**20),
    )(gathered)


def solution(mesh):
    return jax.shard_map(
        on_device,
        mesh=mesh,
        in_specs=(
            P(("grp", "dp"), None),
            P(("grp", "dp"), None),
            P(("grp", "dp"), None, None),
            P(("grp", "dp"), None),
        ),
        out_specs=P(),
        check_vma=False,
    )
```

time: 258 us -> 57.9 us (0.22)
  waiting for transfers between devices: 156 us -> 0 us
  Pallas kernels: 0 us -> 56.9 us
  local copies, waits for them, and re-layouts: 41 us -> 0.89 us
  other arithmetic: 32.6 us -> 0 us
  matrix products: 14.4 us -> 0 us
  between operations: 13.4 us -> 0.01 us
    psum x1 -> x0, waiting for transfers between devices: 156 us -> none  [on_device(): lax.psum(own.astype(jnp.bfloat16), ('grp', 'dp')).astype(jnp.float32)]
    pallas_call x0 -> x2, Pallas kernels: none -> 56.9 us  [the longest x1 53.3 us: on_device(): pl.pallas_call(reduce_kernel, out_shape=jax.ShapeDtypeStruct(shape, bf16)...]
    div x4 -> x0, local copies, waits for them, and re-layouts: 23.1 us -> none  [quantize(): blocks / scales.astype(jnp.float32)[..., None]]
    abs x2 -> x0, local copies, waits for them, and re-layouts: 16.3 us -> none  [quantize(): largest = jnp.max(jnp.abs(blocks), axis=-1)]
    mul x2 -> x0, other arithmetic: 14.9 us -> none  [dequantize(): blocks * scales.astype(jnp.float32)[..., None]]
    dot_general x1 -> x0, matrix products: 14.4 us -> none  [on_device(): lax.dot_general(activations, cotangent, (((0,), (0,)), ((), ())), preferr...]
    reduce_max x2 -> x0, other arithmetic: 6.56 us -> none  [quantize(): largest = jnp.max(jnp.abs(blocks), axis=-1)]
    abs x1 -> x0, other arithmetic: 5.29 us -> none  [quantize(): largest = jnp.max(jnp.abs(blocks), axis=-1)]
  transfers between devices with their start and end apart: 1 -> 0, of which waited for: 1 -> 0; matrix products, arithmetic and copies ran while one was open for 0% -> 0% of each run, Pallas kernels for 0% -> 0%
where the time goes in v2:
time: 57.9 us; the launch traced here: 57.8 us
  Pallas kernels  56.9 us (98%)
  local copies, waits for them, and re-layouts  0.89 us (2%)
    pallas_call x1, Pallas kernels, on_device(): pl.pallas_call(reduce_kernel, out_shape=jax.ShapeDtypeStruct(shape, bf16)...  53.3 us
    pallas_call x1, Pallas kernels, on_device(): pl.pallas_call(expand_kernel, grid=(B,), in_specs=[pl.BlockSpec((2, 1, 3,...  3.61 us

profile of v2, /device:TPU:1, one launch (start us, length us, event | category | flops | bytes accessed | tf_op | source)
XLA Modules:
  0.0 57.8 jit_solution(6838512890323173705)
XLA Ops:
  0.0 0.0 copy-start
  0.0 0.9 %copy-done = f32[10,1280]{1,0:T(8,128)S(1)} copy-done((f32[10,1280]{1,0:T(8,128)S(1)}, f32[10,1280]{1,0:T(8,128)}, u32[]{:S(2)}) %copy-start) | copy-done | bytes 51224
  0.9 53.3 %shard_map.46.g_ref = bf16[2,5,3,4,16,8,128]{6,5,4,3,2,1,0:T(8,128)(2,1)S(1)} custom-call(bf16[2048,1280]{1,0:T(8,128)(2,1)} %a_hbm.1, bf16[2048,1280]{1,0:T(8,128)(2,1)} %c_hbm.1, f32[1,1280,1280]{2,1,0:T(8,128)} %e_hbm.1, f32[10,1280]{1,0:T(8,128)S(1)} %copy-done), custom_call_target="tpu_custom_call" | custom-call | tf_op jit(solution)/shard_map/pallas_call | solution.py:267
  54.2 3.6 %shard_map.47 = f32[1280,1280]{1,0:T(8,128)} custom-call(bf16[2,5,3,4,16,8,128]{6,5,4,3,2,1,0:T(8,128)(2,1)S(1)} %shard_map.46.g_ref), custom_call_target="tpu_custom_call" | custom-call | tf_op jit(solution)/shard_map/pallas_call | solution.py:293
Async XLA Ops:
  0.0 0.9 %copy-start = (f32[10,1280]{1,0:T(8,128)S(1)}, f32[10,1280]{1,0:T(8,128)}, u32[]{:S(2)}) copy-start(f32[10,1280]{1,0:T(8,128)} %oe_ref.1) | copy-start | bytes 153604

commit v3 on v2

v3 whole, which is shorter than its diff:
```python
import jax
import jax.numpy as jnp
from jax import lax
from jax.experimental import pallas as pl
from jax.experimental.pallas import tpu as pltpu
from jax.sharding import PartitionSpec as P

D = 1280
BLOCK = 128
TOK = 2048
MESH = pl.DeviceIdType.MESH
B = 5
ROWS = D // B
TILES = ROWS // 8
HALF = 5
CHUNKS = 5
WIDE = D // CHUNKS
KS = (3, 3, 2)
OFFS = (0, 12, 24)
KOFF = (0, 3, 6)
ORDER = (("z", "y", "x"), ("y", "x", "z"), ("x", "z", "y"))
PLANE = [(i, j) for i in (2, 1, 3, 0) for j in (2, 1, 3, 0) if i or j]
GROUPS = ((0, 2), (2, 2), (4, 1))


def quantized(x):
    largest = jnp.max(jnp.abs(x), axis=-1, keepdims=True)
    scale = ((largest + 1e-06) / 127.0).astype(jnp.bfloat16).astype(jnp.float32)
    level = (x * (1.0 / scale)).astype(jnp.bfloat16).astype(jnp.float32)
    return level * scale


def places():
    g, d = lax.axis_index("grp"), lax.axis_index("dp")
    return {
        "core": lax.rem(g, 2),
        "z": 2 * (d // 16) + g // 2,
        "y": lax.rem(d // 4, 4),
        "x": lax.rem(d, 4),
    }


def device_at(place):
    z = place["z"]
    return (2 * lax.rem(z, 2) + place["core"], 16 * (z // 2) + 4 * place["y"] + place["x"])


def along(place, axis, step):
    return {**place, axis: lax.rem(place[axis] + step, 4)}


def across(place, c, steps):
    return along(along(place, ORDER[c][1], steps[0]), ORDER[c][2], steps[1])


def reduce_kernel(
    a_hbm, c_hbm, e_hbm, oe_hbm, g_ref,
    a_v, c_v, e_v, oe_v, at_0, at_1, pad_v, q, rx0, s, r1, t, r2,
    a_sem, c_sem, e_sem, oe_sem, d2d_recv, p1_recv, p2_recv, g2_recv, g1_recv, gd_recv, sent,
):
    me = places()
    core = me["core"]
    partner = {**me, "core": 1 - core}
    slot = [4 * me[ORDER[c][1]] + me[ORDER[c][2]] for c in range(3)]

    def load_a(b):
        return pltpu.make_async_copy(a_hbm.at[:, pl.ds(b * ROWS, ROWS)], a_v.at[b], a_sem.at[b])

    def load_e(b):
        return pltpu.make_async_copy(e_hbm.at[0, pl.ds(b * ROWS, ROWS), :], e_v.at[b], e_sem.at[b])

    def columns(n):
        return pl.ds(n * WIDE, WIDE)

    def load_c(n):
        return pltpu.make_async_copy(c_hbm.at[:, columns(n)], c_v.at[:, columns(n)], c_sem.at[n])

    load_a(0).start()
    load_c(0).start()
    load_oe = pltpu.make_async_copy(oe_hbm, oe_v, oe_sem)
    load_oe.start()

    peers = [partner] + [along(me, axis, step) for axis in "xyz" for step in (1, 2, 3)]
    peers += [across(me, c, steps) for c in range(3) for steps in PLANE if steps[0] and steps[1]]
    barrier = pltpu.get_barrier_semaphore()
    for peer in peers:
        pl.semaphore_signal(barrier, inc=1, device_id=device_at(peer), device_id_type=MESH)

    load_c(1).start()
    load_c(2).start()
    load_e(0).start()

    def push(src, dst, peer, send, recv):
        pltpu.make_async_remote_copy(
            src_ref=src, dst_ref=dst, send_sem=send, recv_sem=recv,
            device_id=device_at(peer), device_id_type=MESH,
        ).start()

    def landed(ref, sem):
        pltpu.make_async_copy(ref, ref, sem).wait()

    index = lax.axis_index("grp") * 32 + lax.axis_index("dp")
    first_tile = (10 * index) // 8
    shift = 10 * index - 8 * first_tile
    load_oe.wait()
    row = lax.broadcasted_iota(jnp.int32, (16, D), 0)
    padded = jnp.zeros((16, D), jnp.float32)
    for r in range(10):
        padded = jnp.where(row == shift + r, oe_v[r : r + 1, :], padded)
    for h in range(2):
        for j in range(HALF):
            for w in range(2):
                col = (h * HALF + j) * 128
                pad_v[h, w, j] = padded[8 * w : 8 * w + 8, col : col + 128]

    def add_owner_error(b, half):
        for w in range(2):
            tile = first_tile + w
            i = lax.rem(tile, TILES)
            extra = jnp.where(tile // TILES == b, pad_v[half, w], 0.0)
            q[b, half, i] = (q[b, half, i].astype(jnp.float32) + extra).astype(jnp.bfloat16)

    def multiply(b, n, at_v):
        x = jnp.dot(at_v[...], c_v[:, columns(n)], preferred_element_type=jnp.float32)
        x = x + e_v[b, :, columns(n)]
        for u in range(2):
            at = 2 * n + u
            own = quantized(x[:, u * 128 : (u + 1) * 128])
            q[b, at // HALF, :, at % HALF] = own.astype(jnp.bfloat16).reshape(TILES, 8, 128)

    def to_partner(b):
        for half in range(2):
            add_owner_error(b, half)
        push(q.at[b, 1 - core], rx0.at[b], partner, sent.at[0], d2d_recv.at[b])

    def chip_sum(b):
        landed(rx0.at[b], d2d_recv.at[b])
        s[b] = (q[b, core].astype(jnp.float32) + rx0[b].astype(jnp.float32)).astype(jnp.bfloat16)
        for step in (2, 1, 3):
            for c in range(3):
                peer = along(me, ORDER[c][0], step)
                at = OFFS[c] + peer[ORDER[c][0]] * KS[c]
                push(
                    s.at[b, pl.ds(at, KS[c])], r1.at[b, step - 1, pl.ds(KOFF[c], KS[c])],
                    peer, sent.at[1], p1_recv.at[b],
                )

    def first_sum(b):
        landed(r1.at[b], p1_recv.at[b])
        for c in range(3):
            total = s[b, pl.ds(OFFS[c] + me[ORDER[c][0]] * KS[c], KS[c])].astype(jnp.float32)
            for step in range(3):
                total = total + r1[b, step, KOFF[c] : KOFF[c] + KS[c]].astype(jnp.float32)
            t[b, c, 0 : 5 * KS[c]] = total.astype(jnp.bfloat16).reshape(5 * KS[c], 8, 128)

    def plane_send(i):
        b, nb = GROUPS[i]
        for k, steps in enumerate(PLANE):
            for c in range(3):
                peer = across(me, c, steps)
                at = 4 * peer[ORDER[c][1]] + peer[ORDER[c][2]]
                push(
                    t.at[pl.ds(b, nb), c, at], r2.at[pl.ds(b, nb), c, k],
                    peer, sent.at[2], p2_recv.at[i],
                )

    def own_update(i):
        b, nb = GROUPS[i]
        landed(r2.at[pl.ds(b, nb)], p2_recv.at[i])
        for c in range(3):
            total = t[b : b + nb, c, slot[c]].astype(jnp.float32)
            for k in range(15):
                total = total + r2[b : b + nb, c, k].astype(jnp.float32)
            g_ref[core, b : b + nb, c, me[ORDER[c][0]], slot[c]] = quantized(total).astype(jnp.bfloat16)
        for steps in PLANE:
            for c in range(3):
                ref = g_ref.at[core, pl.ds(b, nb), c, me[ORDER[c][0]], slot[c]]
                push(ref, ref, across(me, c, steps), sent.at[3], g2_recv.at[i])

    def piece(i, c, place):
        b, nb = GROUPS[i]
        return g_ref.at[core, pl.ds(b, nb), c, place, pl.ds(0, 5 * KS[c])]

    def forward(i, step):
        for c in range(3):
            ref = piece(i, c, lax.rem(me[ORDER[c][0]] + 4 - step, 4))
            push(ref, ref, partner, sent.at[5], gd_recv.at[i])

    def spread(i):
        b, nb = GROUPS[i]
        landed(r2.at[pl.ds(b, nb)], g2_recv.at[i])
        for step in (2, 1, 3):
            for c in range(3):
                ref = piece(i, c, me[ORDER[c][0]])
                push(ref, ref, along(me, ORDER[c][0], step), sent.at[4], g1_recv.at[i, step - 1])
        forward(i, 0)

    def pass_on(i):
        b, nb = GROUPS[i]
        for step in (1, 3, 2):
            landed(r1.at[pl.ds(b, nb), 0], g1_recv.at[i, step - 1])
            forward(i, step)

    load_a(0).wait()
    load_c(3).start()
    load_c(4).start()
    load_a(1).start()
    at_0[...] = a_v[0].T
    for n in range(3):
        load_c(n).wait()
    load_e(0).wait()
    load_e(1).start()
    load_a(2).start()
    for n in range(3):
        multiply(0, n, at_0)
    load_c(3).wait()
    load_c(4).wait()
    load_e(2).start()
    load_a(3).start()
    for n in range(3, CHUNKS):
        multiply(0, n, at_0)
    pl.semaphore_wait(barrier, len(peers))
    to_partner(0)

    def block(b, at_v):
        load_a(b).wait()
        load_e(b).wait()

        @pl.when(b < B - 2)
        def _():
            load_e(b + 2).start()

        @pl.when(b < B - 3)
        def _():
            load_a(b + 3).start()

        at_v[...] = a_v[b].T
        for n in range(CHUNKS):
            multiply(b, n, at_v)
        to_partner(b)
        chip_sum(b - 1)

    def pair(k, carry):
        block(2 * k + 1, at_1)
        block(2 * k + 2, at_0)
        return carry

    lax.fori_loop(0, (B - 1) // 2, pair, 0)
    first_sum(0)
    first_sum(1)
    plane_send(0)
    chip_sum(B - 1)
    first_sum(2)
    first_sum(3)
    plane_send(1)
    first_sum(4)
    plane_send(2)
    own_update(0)
    own_update(1)
    own_update(2)
    spread(0)
    spread(1)
    pass_on(0)
    spread(2)
    pass_on(1)
    pass_on(2)
    for i, (b, nb) in enumerate(GROUPS):
        landed(rx0.at[pl.ds(b, nb)], gd_recv.at[i])
    landed(rx0, sent.at[0])
    landed(r1, sent.at[1])
    landed(r2, sent.at[2])
    landed(r2, sent.at[3])
    landed(r1, sent.at[4])
    landed(rx0, sent.at[5])


def expand_kernel(g_ref, out_hbm, rows_v, sem):
    copies = []
    for b in range(B):
        for h in range(2):
            for c in range(3):
                for a in range(4):
                    for k in range(KS[c]):
                        row = 8 * (OFFS[c] + a * KS[c] + k)
                        for j in range(HALF):
                            col = (h * HALF + j) * 128
                            rows_v[b, row : row + 8, col : col + 128] = g_ref[h, b, c, a, 5 * k + j].astype(jnp.float32)
        copies.append(pltpu.make_async_copy(rows_v.at[b], out_hbm.at[pl.ds(b * ROWS, ROWS)], sem.at[b]))
        copies[-1].start()
    for copy in copies:
        copy.wait()


def on_device(activations, cotangent, carried_error, owner_error):
    any_spec = pl.BlockSpec(memory_space=pltpu.HBM)
    bf16, f32, dma = jnp.bfloat16, jnp.float32, pltpu.SemaphoreType.DMA
    shape = (2, B, 3, 4, 16, 8, 128)
    ng = len(GROUPS)
    gathered = pl.pallas_call(
        reduce_kernel,
        out_shape=jax.ShapeDtypeStruct(shape, bf16),
        in_specs=[any_spec] * 4,
        out_specs=pl.BlockSpec(memory_space=pltpu.VMEM),
        scratch_shapes=[
            pltpu.VMEM((B, TOK, ROWS), bf16),
            pltpu.VMEM((TOK, D), bf16),
            pltpu.VMEM((B, ROWS, D), f32),
            pltpu.VMEM((10, D), f32),
            pltpu.VMEM((ROWS, TOK), bf16),
            pltpu.VMEM((ROWS, TOK), bf16),
            pltpu.VMEM((2, 2, HALF, 8, 128), f32),
            pltpu.VMEM((B, 2, TILES, HALF, 8, 128), bf16),
            pltpu.VMEM((B, TILES, HALF, 8, 128), bf16),
            pltpu.VMEM((B, TILES, HALF, 8, 128), bf16),
            pltpu.VMEM((B, 3, 8, HALF, 8, 128), bf16),
            pltpu.VMEM((B, 3, 16, 8, 128), bf16),
            pltpu.VMEM((B, 3, 15, 8, 128), bf16),
            dma((B,)), dma((CHUNKS,)), dma((B,)), dma, dma((B,)), dma((B,)),
            dma((ng,)), dma((ng,)), dma((ng, 3)), dma((ng,)), dma((6,)),
        ],
        compiler_params=pltpu.CompilerParams(
            collective_id=0, has_side_effects=True, vmem_limit_bytes=48 * 2**20
        ),
    )(*(pltpu.with_memory_space_constraint(v, pltpu.HBM) for v in (activations, cotangent, carried_error, owner_error)))
    return pl.pallas_call(
        expand_kernel,
        in_specs=[pl.BlockSpec(memory_space=pltpu.VMEM)],
        out_specs=any_spec,
        out_shape=jax.ShapeDtypeStruct((D, D), f32),
        scratch_shapes=[pltpu.VMEM((B, ROWS, D), f32), dma((B,))],
        compiler_params=pltpu.CompilerParams(vmem_limit_bytes=16 * 2**20),
    )(gathered)


def solution(mesh):
    return jax.shard_map(
        on_device,
        mesh=mesh,
        in_specs=(
            P(("grp", "dp"), None),
            P(("grp", "dp"), None),
            P(("grp", "dp"), None, None),
            P(("grp", "dp"), None),
        ),
        out_specs=P(),
        check_vma=False,
    )
```

time: 57.9 us -> 46.8 us (0.81)
  Pallas kernels: 56.9 us -> 46.7 us
  local copies, waits for them, and re-layouts: 0.89 us -> 0 us
    pallas_call x1, Pallas kernels: 53.3 us -> 43.8 us  [on_device(): pl.pallas_call(reduce_kernel, out_shape=jax.ShapeDtypeStruct(shape, bf16)...]
    unnamed x2 -> x0, local copies, waits for them, and re-layouts: 0.89 us -> none
    pallas_call x1, Pallas kernels: 3.61 us -> 2.91 us  [on_device(): pl.pallas_call(expand_kernel, in_specs=[pl.BlockSpec(memory_space=pltpu.V...]
where the time goes in v3:
time: 46.8 us; the launch traced here: 46.7 us
  Pallas kernels  46.7 us (100%)
    pallas_call x1, Pallas kernels, on_device(): pl.pallas_call(reduce_kernel, out_shape=jax.ShapeDtypeStruct(shape, bf16)...  43.8 us
    pallas_call x1, Pallas kernels, on_device(): pl.pallas_call(expand_kernel, in_specs=[pl.BlockSpec(memory_space=pltpu.V...  2.91 us

profile of v3, /device:TPU:1, one launch (start us, length us, event | category | flops | bytes accessed | tf_op | source)
XLA Modules:
  0.0 46.7 jit_solution(18079994736433560471)
XLA Ops:
  0.0 43.8 %shard_map.46.g_ref = bf16[2,5,3,4,16,8,128]{6,5,4,3,2,1,0:T(8,128)(2,1)S(1)} custom-call(bf16[2048,1280]{1,0:T(8,128)(2,1)} %a_hbm.1, bf16[2048,1280]{1,0:T(8,128)(2,1)} %c_hbm.1, f32[1,1280,1280]{2,1,0:T(8,128)} %e_hbm.1, f32[10,1280]{1,0:T(8,128)} %oe_hbm.1), custom_call_target="tpu_custom_call" | custom-call | tf_op jit(solution)/shard_map/pallas_call | solution.py:299
  43.8 2.9 %shard_map.47 = f32[1280,1280]{1,0:T(8,128)} custom-call(bf16[2,5,3,4,16,8,128]{6,5,4,3,2,1,0:T(8,128)(2,1)S(1)} %shard_map.46.g_ref), custom_call_target="tpu_custom_call" | custom-call | tf_op jit(solution)/shard_map/pallas_call | solution.py:325

commit v4 on v3

--- a/solution.py
+++ b/solution.py
@@ -20,7 +20,7 @@
 KOFF = (0, 3, 6)
 ORDER = (("z", "y", "x"), ("y", "x", "z"), ("x", "z", "y"))
 PLANE = [(i, j) for i in (2, 1, 3, 0) for j in (2, 1, 3, 0) if i or j]
-GROUPS = ((0, 2), (2, 2), (4, 1))
+GROUPS = ((0, 3), (3, 2))
 
 
 def quantized(x):
@@ -81,7 +81,6 @@
     load_oe.start()
 
     peers = [partner] + [along(me, axis, step) for axis in "xyz" for step in (1, 2, 3)]
-    peers += [across(me, c, steps) for c in range(3) for steps in PLANE if steps[0] and steps[1]]
     barrier = pltpu.get_barrier_semaphore()
     for peer in peers:
         pl.semaphore_signal(barrier, inc=1, device_id=device_at(peer), device_id_type=MESH)
@@ -219,10 +218,8 @@
     load_a(3).start()
     for n in range(3, CHUNKS):
         multiply(0, n, at_0)
-    pl.semaphore_wait(barrier, len(peers))
-    to_partner(0)
-
-    def block(b, at_v):
+
+    def block(b):
         load_a(b).wait()
         load_e(b).wait()
 
@@ -234,36 +231,41 @@
         def _():
             load_a(b + 3).start()
 
-        at_v[...] = a_v[b].T
+        at_1[...] = a_v[b].T
         for n in range(CHUNKS):
-            multiply(b, n, at_v)
+            multiply(b, n, at_1)
+
+    block(1)
+    pl.semaphore_wait(barrier, len(peers))
+    to_partner(0)
+    to_partner(1)
+
+    def step(b, carry):
+        block(b)
         to_partner(b)
+
+        @pl.when(b == 2)
+        def _():
+            chip_sum(0)
+
         chip_sum(b - 1)
-
-    def pair(k, carry):
-        block(2 * k + 1, at_1)
-        block(2 * k + 2, at_0)
         return carry
 
-    lax.fori_loop(0, (B - 1) // 2, pair, 0)
+    lax.fori_loop(2, B, step, 0)
     first_sum(0)
     first_sum(1)
-    plane_send(0)
     chip_sum(B - 1)
     first_sum(2)
+    plane_send(0)
     first_sum(3)
+    first_sum(4)
     plane_send(1)
-    first_sum(4)
-    plane_send(2)
     own_update(0)
     own_update(1)
-    own_update(2)
     spread(0)
     spread(1)
     pass_on(0)
-    spread(2)
     pass_on(1)
-    pass_on(2)
     for i, (b, nb) in enumerate(GROUPS):
         landed(rx0.at[pl.ds(b, nb)], gd_recv.at[i])
     landed(rx0, sent.at[0])

time: 46.8 us -> 46.1 us (0.985)
  Pallas kernels: 46.7 us -> 46 us
    pallas_call x1, Pallas kernels: 43.8 us -> 43.1 us  [on_device(): pl.pallas_call(reduce_kernel, out_shape=jax.ShapeDtypeStruct(shape, bf16)...]
where the time goes in v4:
time: 46.1 us; the launch traced here: 46 us
  Pallas kernels  46 us (100%)
    pallas_call x1, Pallas kernels, on_device(): pl.pallas_call(reduce_kernel, out_shape=jax.ShapeDtypeStruct(shape, bf16)...  43.1 us
    pallas_call x1, Pallas kernels, on_device(): pl.pallas_call(expand_kernel, in_specs=[pl.BlockSpec(memory_space=pltpu.V...  2.91 us

profile of v4, /device:TPU:1, one launch (start us, length us, event | category | flops | bytes accessed | tf_op | source)
XLA Modules:
  0.0 46.0 jit_solution(2667783703187286724)
XLA Ops:
  0.0 43.1 %shard_map.46.g_ref = bf16[2,5,3,4,16,8,128]{6,5,4,3,2,1,0:T(8,128)(2,1)S(1)} custom-call(bf16[2048,1280]{1,0:T(8,128)(2,1)} %a_hbm.1, bf16[2048,1280]{1,0:T(8,128)(2,1)} %c_hbm.1, f32[1,1280,1280]{2,1,0:T(8,128)} %e_hbm.1, f32[10,1280]{1,0:T(8,128)} %oe_hbm.1), custom_call_target="tpu_custom_call" | custom-call | tf_op jit(solution)/shard_map/pallas_call | solution.py:301
  43.1 2.9 %shard_map.47 = f32[1280,1280]{1,0:T(8,128)} custom-call(bf16[2,5,3,4,16,8,128]{6,5,4,3,2,1,0:T(8,128)(2,1)S(1)} %shard_map.46.g_ref), custom_call_target="tpu_custom_call" | custom-call | tf_op jit(solution)/shard_map/pallas_call | solution.py:327

commit v5 on v4

--- a/solution.py
+++ b/solution.py
@@ -19,7 +19,8 @@
 OFFS = (0, 12, 24)
 KOFF = (0, 3, 6)
 ORDER = (("z", "y", "x"), ("y", "x", "z"), ("x", "z", "y"))
-PLANE = [(i, j) for i in (2, 1, 3, 0) for j in (2, 1, 3, 0) if i or j]
+PLANE = [(i, j) for i in range(4) for j in range(4) if i or j]
+PLANE.sort(key=lambda at: -(at[0] % 2 + at[1] % 2 + 2 * (at[0] == 2) + 2 * (at[1] == 2)))
 GROUPS = ((0, 3), (3, 2))
 
 

time: 46.1 us -> 45.9 us (level)
  no operation moved by 1% of the time
where the time goes in v5:
time: 45.9 us; the launch traced here: 45.8 us
  Pallas kernels  45.8 us (100%)
    pallas_call x1, Pallas kernels, on_device(): pl.pallas_call(reduce_kernel, out_shape=jax.ShapeDtypeStruct(shape, bf16)...  42.9 us
    pallas_call x1, Pallas kernels, on_device(): pl.pallas_call(expand_kernel, in_specs=[pl.BlockSpec(memory_space=pltpu.V...  2.91 us

profile of v5, /device:TPU:1, one launch (start us, length us, event | category | flops | bytes accessed | tf_op | source)
XLA Modules:
  0.0 45.8 jit_solution(9446375593178226433)
XLA Ops:
  0.0 42.9 %shard_map.46.g_ref = bf16[2,5,3,4,16,8,128]{6,5,4,3,2,1,0:T(8,128)(2,1)S(1)} custom-call(bf16[2048,1280]{1,0:T(8,128)(2,1)} %a_hbm.1, bf16[2048,1280]{1,0:T(8,128)(2,1)} %c_hbm.1, f32[1,1280,1280]{2,1,0:T(8,128)} %e_hbm.1, f32[10,1280]{1,0:T(8,128)} %oe_hbm.1), custom_call_target="tpu_custom_call" | custom-call | tf_op jit(solution)/shard_map/pallas_call | solution.py:302
  42.9 2.9 %shard_map.47 = f32[1280,1280]{1,0:T(8,128)} custom-call(bf16[2,5,3,4,16,8,128]{6,5,4,3,2,1,0:T(8,128)(2,1)S(1)} %shard_map.46.g_ref), custom_call_target="tpu_custom_call" | custom-call | tf_op jit(solution)/shard_map/pallas_call | solution.py:328
